TPU v7x, 128 devices: a whole 4x4x4 slice. The times are simulated.
128 devices in a mesh: row: 16 (over y_hi, x, core), col: 8 (over z, y_lo).
Axes of the slice: x: 4, y: 4 (y_hi: 2, y_lo: 2; y = y_hi * 2 + y_lo), z: 4, core: 2. Of those that a mesh axis runs over, the one named last changes fastest.
Arguments:
- residual: bfloat16 [16, 8, 2048, 512], P('row', 'col'), may hold values from -6 to 6
- self_tiles: bfloat16 [16, 8, 2048, 2048], P('row', 'col'), may hold values from -0.09375 to 0.09375
- side_tiles: bfloat16 [16, 8, 2048, 2048], P('row', 'col'), may hold values from -0.09375 to 0.09375
- row_cluster_basis: bfloat16 [16, 8, 2048, 32], P('row', 'col'), may hold values from -0.125 to 0.125
- column_cluster_basis: bfloat16 [16, 8, 2048, 32], P('row', 'col'), may hold values from -1 to 1
- couplings: bfloat16 [16, 8, 64, 32, 32], P('row', 'col'), may hold values from -0.1875 to 0.1875
- near_side: int32 [16, 8], P('row', 'col'), may hold values from -1 to 1
- adm_targets: int32 [16, 8, 64], P('row', 'col'), may hold values from 0 to 127, as said below
- adm_ranks: int32 [16, 8, 64], P('row', 'col'), may hold values from 8 to 32
- adm_count: int32 [16, 8], P('row', 'col'), may hold values from 1 to 64
Outputs:
- gradient: float32 [16, 8, 2048, 512], P('row', 'col')
Inputs may be any that keep to these rules, and one draw needn't show every extreme that they name: `near_side`: -1 or +1 names the cluster row before or after around the loop of 16 rows; 0 means no such tile. Each entry of adm_targets for the block row of linear index i is the linear index of a cluster other than i; slot 0 names i - 1 or i + 1, counted round the 128 clusters; targets may repeat.
All inputs are finite; a program needn't handle non-finite values.
Results may differ from a plain program's by a relative error of at most 0.0033.
Values may be sent and summed in bfloat16 or wider, within the bound.
A program may use at most 128 MiB of HBM per device.

v0:
```python
import jax
import jax.numpy as jnp
from jax import lax
from jax.sharding import Mesh
from jax.sharding import PartitionSpec as P

ROW = ("row_0", "row_1", "row_2")
COL = ("col_0", "col_1")
ROW_COL = ("row_0", "row_1", "row_2", "col_0", "col_1")


def with_halo(block, sides, width):
    for axis, dim in sides:
        count = lax.axis_size(axis)
        forward = [(i, i + 1) for i in range(count - 1)]
        forward.append((count - 1, 0))
        backward = [(target, source) for source, target in forward]
        low = lax.ppermute(
            lax.slice_in_dim(block, block.shape[dim] - width, None, axis=dim), axis, forward
        )
        high = lax.ppermute(lax.slice_in_dim(block, 0, width, axis=dim), axis, backward)
        block = jnp.concatenate([low, block, high], axis=dim)
    return block


def cut_rows(length, count):
    unit = 8 if length >= 8 * count else 1
    return [length // unit * k // count * unit for k in range(1, count)]


def all_blocks(value, axes, sequence):
    pieces = value[None]
    for k in sequence:
        pieces = lax.all_gather(pieces, axes[k], axis=0, tiled=True)
    held = [lax.axis_size(axes[k]) for k in reversed(sequence)]
    pieces = pieces.reshape(*held, *value.shape)
    turned = sorted(range(len(sequence)), key=lambda place: sequence[len(sequence) - 1 - place])
    return pieces.transpose(*turned, *range(len(sequence), pieces.ndim)).reshape(-1, *value.shape)


def in_order(pieces, dim):
    pieces = jnp.moveaxis(pieces, 0, dim)
    dims = pieces.shape
    return pieces.reshape(*dims[:dim], dims[dim] * dims[dim + 1], *dims[dim + 2 :])


def gather_at_once(value, axes, dim):
    split_at = max(range(max(1, value.ndim - 1)), key=lambda d: value.shape[d])
    count, done = (len(axes), [])
    for initial, slab in enumerate(
        jnp.split(value, cut_rows(value.shape[split_at], count), axis=split_at)
    ):
        if slab.size:
            sequence = [(initial - k) % count for k in range(count)]
            done.append(all_blocks(slab, axes, sequence))
    return in_order(jnp.concatenate(done, axis=split_at + 1), dim)


def contract(tile, values):
    return lax.dot_general(
        tile, values, (((0,), (0,)), ((), ())), preferred_element_type=jnp.float32
    )


def on_device(
    residual,
    self_tiles,
    side_tiles,
    row_cluster_basis,
    column_cluster_basis,
    couplings,
    near_side,
    adm_targets,
    adm_ranks,
    adm_count,
):
    slot_count = couplings.shape[2]
    rank_dimension = couplings.shape[3]
    cluster_groups = lax.axis_size(ROW) * lax.axis_size(COL)
    local_rows = residual[0, 0]
    coefficient_table = contract(row_cluster_basis[0, 0], local_rows).astype(jnp.bfloat16)
    rank_index = jnp.arange(rank_dimension, dtype=jnp.int32)
    slot_index = jnp.arange(slot_count, dtype=jnp.int32)
    keep_mask = (rank_index[None, :] < adm_ranks[0, 0][:, None]) & (slot_index < adm_count[0, 0])[
        :, None
    ]
    keep_float = keep_mask.astype(jnp.float32)
    masked = couplings[0, 0].astype(jnp.float32) * keep_float[:, :, None] * keep_float[:, None, :]
    onehot = (
        adm_targets[0, 0][:, None] == jnp.arange(cluster_groups, dtype=jnp.int32)[None, :]
    ).astype(jnp.float32)
    coupled_blocks = lax.dot_general(
        onehot,
        masked.reshape(slot_count, rank_dimension * rank_dimension),
        (((0,), (0,)), ((), ())),
        precision=lax.Precision.HIGHEST,
        preferred_element_type=jnp.float32,
    )
    coupled_blocks = coupled_blocks.reshape(cluster_groups, rank_dimension, rank_dimension)
    padded = with_halo(residual, ((ROW, 0),), 1)
    side_offset = near_side[0, 0]
    neighbour = lax.dynamic_index_in_dim(padded, side_offset + 1, 0, keepdims=False)[0]
    own_part = contract(self_tiles[0, 0], local_rows)
    side_part = contract(side_tiles[0, 0], neighbour) * (side_offset != 0).astype(jnp.float32)
    received = lax.all_to_all(
        coupled_blocks.astype(jnp.bfloat16), ROW_COL, split_axis=0, concat_axis=0, tiled=True
    ).astype(coupled_blocks.dtype)
    dual_sums = jnp.einsum(
        "cab,can->bn",
        received,
        gather_at_once(coefficient_table[None], ROW_COL, 0).astype(jnp.float32),
        precision=lax.Precision.HIGHEST,
    )
    dual_vector = dual_sums.astype(jnp.bfloat16)
    distant_part = jnp.dot(
        column_cluster_basis[0, 0], dual_vector, preferred_element_type=jnp.float32
    )
    gradient = own_part + side_part + distant_part
    return gradient[None, None]


def solution(mesh):
    torus = Mesh(mesh.devices.reshape(2, 4, 2, 4, 2), ("row_0", "row_1", "row_2", "col_0", "col_1"))
    in_specs = (
        P(ROW, COL, None, None),
        P(ROW, COL, None, None),
        P(ROW, COL, None, None),
        P(ROW, COL, None, None),
        P(ROW, COL, None, None),
        P(ROW, COL, None, None, None),
        P(ROW, COL),
        P(ROW, COL, None),
        P(ROW, COL, None),
        P(ROW, COL),
    )
    out_specs = P(ROW, COL, None, None)
    return jax.shard_map(
        on_device, mesh=torus, in_specs=in_specs, out_specs=out_specs, check_vma=False
    )
```

profile of v0, /device:TPU:40, one launch (start us, length us, event | category | flops | bytes accessed | tf_op | source)
XLA Modules:
  0.0 274.3 jit_solution(9813288460616339119)
XLA Ops:
  0.0 0.0 copy-start
  0.0 0.0 collective-permute-start
  0.0 5.3 %collective-permute-start.1 = (bf16[1,1,2048,512]{3,2,1,0:T(8,128)(2,1)}, bf16[1,1,2048,512]{3,2,1,0:T(8,128)(2,1)}, u32[]{:S(2)}, u32[]{:S(2)}) collective-permute-start(bf16[1,1,2048,512]{3,2,1,0:T(8,128)(2,1)} %param.10), channel_id=1, source_target_pairs={{8,0},{16,8},{24,16},{32,24},{40,32},{48,40},{56,48},{64,56},{72,6... | collective-permute-start | bytes 6291464 | tf_op jit(solution)/shard_map/ppermute | solution.py:21
  6.0 0.7 fusion.37
  6.7 1.0 fusion.29
  7.7 1.1 convolution_convert_fusion
  8.8 1.4 copy.40
  10.2 1.5 reshape.163
  11.8 8.2 %all-to-all-start = ((bf16[128,2,512]{2,1,0:T(2,128)(2,1)}), bf16[128,2,512]{2,1,0:T(2,128)(2,1)}, u32[]{:S(2)}, u32[]{:S(2)}) async-start(bf16[128,2,512]{2,1,0:T(2,128)(2,1)} %reshape.163), calls=%async_computation | async-start | bytes 524288 | tf_op jit(solution)/shard_map/all_to_all | solution.py:105
  20.0 0.0 copy-done.1
  20.0 1.4 fusion.25
  21.4 11.0 %all-gather = bf16[2,6,512]{2,1,0:T(8,128)(2,1)S(1)} all-gather(bf16[1,6,512]{2,1,0:T(8,128)(2,1)S(1)} %get-tuple-element.9), channel_id=2, replica_groups=mesh['row_0'=2,'row_1'=4,'row_2'=2,'col_0'=4,'col_1'=2] {'row_0'}, dimensions={0}, use_global_device_ids=true | all-gather | bytes 18432 | tf_op jit(solution)/shard_map/all_gather | solution.py:34
  32.4 4.4 %all-gather.1 = bf16[4,6,512]{2,1,0:T(8,128)(2,1)S(1)} all-gather(bf16[2,6,512]{2,1,0:T(8,128)(2,1)S(1)} %all-gather), channel_id=3, replica_groups=mesh['row_0'=2,'row_1'=4,'row_2'=2,'col_0'=4,'col_1'=2] {'col_1'}, dimensions={0}, use_global_device_ids=true | all-gather | bytes 36864 | tf_op jit(solution)/shard_map/all_gather | solution.py:34
  36.8 12.9 %all-gather.2 = bf16[16,6,512]{2,1,0:T(8,128)(2,1)S(1)} all-gather(bf16[4,6,512]{2,1,0:T(8,128)(2,1)S(1)} %all-gather.1), channel_id=4, replica_groups=mesh['row_0'=2,'row_1'=4,'row_2'=2,'col_0'=4,'col_1'=2] {'col_0'}, dimensions={0}, use_global_device_ids=true | all-gather | bytes 122880 | tf_op jit(solution)/shard_map/all_gather | solution.py:34
  49.7 1.9 all-gather.3
  51.7 16.2 %all-gather.4 = bf16[128,6,512]{2,0,1:T(8,128)(2,1)S(1)} all-gather(bf16[32,6,512]{2,0,1:T(8,128)(2,1)S(1)} %all-gather.3), channel_id=6, replica_groups=mesh['row_0'=2,'row_1'=4,'row_2'=2,'col_0'=4,'col_1'=2] {'row_1'}, dimensions={0}, use_global_device_ids=true | all-gather | bytes 983040 | tf_op jit(solution)/shard_map/all_gather | solution.py:34
  67.8 0.3 reshape.121
  68.1 0.9 copy.63
  69.0 0.3 reshape.122
  69.3 0.9 constant_dynamic-update-slice_fusion.3
  70.2 12.2 %all-gather.5 = bf16[4,6,512]{2,1,0:T(8,128)(2,1)S(1)} all-gather(bf16[1,6,512]{2,1,0:T(8,128)(2,1)S(1)} %get-tuple-element.8), channel_id=7, replica_groups=mesh['row_0'=2,'row_1'=4,'row_2'=2,'col_0'=4,'col_1'=2] {'row_1'}, dimensions={0}, use_global_device_ids=true | all-gather | bytes 30720 | tf_op jit(solution)/shard_map/all_gather | solution.py:34
  82.4 6.1 %all-gather.6 = bf16[8,6,512]{2,1,0:T(8,128)(2,1)S(1)} all-gather(bf16[4,6,512]{2,1,0:T(8,128)(2,1)S(1)} %all-gather.5), channel_id=8, replica_groups=mesh['row_0'=2,'row_1'=4,'row_2'=2,'col_0'=4,'col_1'=2] {'row_0'}, dimensions={0}, use_global_device_ids=true | all-gather | bytes 73728 | tf_op jit(solution)/shard_map/all_gather | solution.py:34
  88.5 4.8 %all-gather.7 = bf16[16,6,512]{2,0,1:T(8,128)(2,1)S(1)} all-gather(bf16[8,6,512]{2,0,1:T(8,128)(2,1)S(1)} %copy.43), channel_id=9, replica_groups=mesh['row_0'=2,'row_1'=4,'row_2'=2,'col_0'=4,'col_1'=2] {'col_1'}, dimensions={0}, use_global_device_ids=true | all-gather | bytes 147456 | tf_op jit(solution)/shard_map/all_gather | solution.py:34
  93.3 12.5 %all-gather.8 = bf16[64,6,512]{2,0,1:T(8,128)(2,1)S(1)} all-gather(bf16[16,6,512]{2,0,1:T(8,128)(2,1)S(1)} %all-gather.7), channel_id=10, replica_groups=mesh['row_0'=2,'row_1'=4,'row_2'=2,'col_0'=4,'col_1'=2] {'col_0'}, dimensions={0}, use_global_device_ids=true | all-gather | bytes 491520 | tf_op jit(solution)/shard_map/all_gather | solution.py:34
  105.8 2.4 all-gather.9
  108.2 0.2 reshape.123
  108.4 0.8 copy.62
  109.2 0.3 reshape.124
  109.5 1.8 all-gather.10
  111.3 11.9 %all-gather.11 = bf16[8,7,512]{2,1,0:T(8,128)(2,1)S(1)} all-gather(bf16[2,7,512]{2,1,0:T(8,128)(2,1)S(1)} %all-gather.10), channel_id=13, replica_groups=mesh['row_0'=2,'row_1'=4,'row_2'=2,'col_0'=4,'col_1'=2] {'row_1'}, dimensions={0}, use_global_device_ids=true | all-gather | bytes 71680 | tf_op jit(solution)/shard_map/all_gather | solution.py:34
  123.2 7.0 %all-gather.12 = bf16[16,7,512]{2,0,1:T(8,128)(2,1)S(1)} all-gather(bf16[8,7,512]{2,0,1:T(8,128)(2,1)S(1)} %copy.45), channel_id=14, replica_groups=mesh['row_0'=2,'row_1'=4,'row_2'=2,'col_0'=4,'col_1'=2] {'row_0'}, dimensions={0}, use_global_device_ids=true | all-gather | bytes 172032 | tf_op jit(solution)/shard_map/all_gather | solution.py:34
  130.1 5.4 %all-gather.13 = bf16[32,7,512]{2,0,1:T(8,128)(2,1)S(1)} all-gather(bf16[16,7,512]{2,0,1:T(8,128)(2,1)S(1)} %all-gather.12), channel_id=15, replica_groups=mesh['row_0'=2,'row_1'=4,'row_2'=2,'col_0'=4,'col_1'=2] {'col_1'}, dimensions={0}, use_global_device_ids=true | all-gather | bytes 344064 | tf_op jit(solution)/shard_map/all_gather | solution.py:34
  135.6 13.9 %all-gather.14 = bf16[128,7,512]{2,0,1:T(8,128)(2,1)S(1)} all-gather(bf16[32,7,512]{2,0,1:T(8,128)(2,1)S(1)} %all-gather.13), channel_id=16, replica_groups=mesh['row_0'=2,'row_1'=4,'row_2'=2,'col_0'=4,'col_1'=2] {'col_0'}, dimensions={0}, use_global_device_ids=true | all-gather | bytes 1146880 | tf_op jit(solution)/shard_map/all_gather | solution.py:34
  149.5 0.3 reshape.125
  149.8 0.9 copy.60
  150.8 0.3 reshape.126
  151.1 11.9 %all-gather.15 = bf16[4,6,512]{2,1,0:T(8,128)(2,1)S(1)} all-gather(bf16[1,6,512]{2,1,0:T(8,128)(2,1)S(1)} %get-tuple-element.7), channel_id=17, replica_groups=mesh['row_0'=2,'row_1'=4,'row_2'=2,'col_0'=4,'col_1'=2] {'col_0'}, dimensions={0}, use_global_device_ids=true | all-gather | bytes 30720 | tf_op jit(solution)/shard_map/all_gather | solution.py:34
  163.0 1.8 all-gather.16
  164.9 12.1 %all-gather.17 = bf16[32,6,512]{2,0,1:T(8,128)(2,1)S(1)} all-gather(bf16[8,6,512]{2,0,1:T(8,128)(2,1)S(1)} %copy.47), channel_id=19, replica_groups=mesh['row_0'=2,'row_1'=4,'row_2'=2,'col_0'=4,'col_1'=2] {'row_1'}, dimensions={0}, use_global_device_ids=true | all-gather | bytes 245760 | tf_op jit(solution)/shard_map/all_gather | solution.py:34
  177.0 8.4 %all-gather.18 = bf16[64,6,512]{2,0,1:T(8,128)(2,1)S(1)} all-gather(bf16[32,6,512]{2,0,1:T(8,128)(2,1)S(1)} %all-gather.17), channel_id=20, replica_groups=mesh['row_0'=2,'row_1'=4,'row_2'=2,'col_0'=4,'col_1'=2] {'row_0'}, dimensions={0}, use_global_device_ids=true | all-gather | bytes 589824 | tf_op jit(solution)/shard_map/all_gather | solution.py:34
  185.5 8.5 %all-gather.19 = bf16[128,6,512]{2,0,1:T(8,128)(2,1)S(1)} all-gather(bf16[64,6,512]{2,0,1:T(8,128)(2,1)S(1)} %all-gather.18), channel_id=21, replica_groups=mesh['row_0'=2,'row_1'=4,'row_2'=2,'col_0'=4,'col_1'=2] {'col_1'}, dimensions={0}, use_global_device_ids=true | all-gather | bytes 1179648 | tf_op jit(solution)/shard_map/all_gather | solution.py:34
  194.0 0.2 reshape.127
  194.2 1.1 copy.61
  195.3 0.3 reshape.128
  195.6 4.4 %all-gather.20 = bf16[2,7,512]{2,1,0:T(8,128)(2,1)S(1)} all-gather(bf16[1,7,512]{2,1,0:T(8,128)(2,1)S(1)} %get-tuple-element.5), channel_id=22, replica_groups=mesh['row_0'=2,'row_1'=4,'row_2'=2,'col_0'=4,'col_1'=2] {'col_1'}, dimensions={0}, use_global_device_ids=true | all-gather | bytes 21504 | tf_op jit(solution)/shard_map/all_gather | solution.py:34
  199.9 11.8 %all-gather.21 = bf16[8,7,512]{2,1,0:T(8,128)(2,1)S(1)} all-gather(bf16[2,7,512]{2,1,0:T(8,128)(2,1)S(1)} %all-gather.20), channel_id=23, replica_groups=mesh['row_0'=2,'row_1'=4,'row_2'=2,'col_0'=4,'col_1'=2] {'col_0'}, dimensions={0}, use_global_device_ids=true | all-gather | bytes 71680 | tf_op jit(solution)/shard_map/all_gather | solution.py:34
  211.8 1.9 all-gather.22
  213.7 13.2 %all-gather.23 = bf16[64,7,512]{2,0,1:T(8,128)(2,1)S(1)} all-gather(bf16[16,7,512]{2,0,1:T(8,128)(2,1)S(1)} %all-gather.22), channel_id=25, replica_groups=mesh['row_0'=2,'row_1'=4,'row_2'=2,'col_0'=4,'col_1'=2] {'row_1'}, dimensions={0}, use_global_device_ids=true | all-gather | bytes 573440 | tf_op jit(solution)/shard_map/all_gather | solution.py:34
  226.9 13.4 %all-gather.24 = bf16[128,7,512]{2,0,1:T(8,128)(2,1)S(1)} all-gather(bf16[64,7,512]{2,0,1:T(8,128)(2,1)S(1)} %all-gather.23), channel_id=26, replica_groups=mesh['row_0'=2,'row_1'=4,'row_2'=2,'col_0'=4,'col_1'=2] {'row_0'}, dimensions={0}, use_global_device_ids=true | all-gather | bytes 1376256 | tf_op jit(solution)/shard_map/all_gather | solution.py:34
  241.0 0.9 constant_dynamic-update-slice_fusion.2
  241.9 1.0 constant_dynamic-update-slice_fusion.1
  242.9 0.9 constant_dynamic-update-slice_fusion
  243.9 10.5 %fusion.2 = f32[2048,512]{1,0:T(8,128)} fusion(bf16[1,1,2048,2048]{3,2,1,0:T(8,128)(2,1)} %param.11, bf16[1,1,2048,512]{3,2,1,0:T(8,128)(2,1)} %param.10), kind=kOutput, calls=%fused_computation.2 | convolution fusion | flops 4294967296 | bytes 14680064 | tf_op jit(solution)/shard_map/dot_general | solution.py:60
  254.3 1.0 bitcast_dynamic-update-slice_fusion
  255.3 0.0 all-to-all-done
  255.3 1.9 reshape.164
  257.3 3.1 %fusion.19 = bf16[32,512]{1,0:T(8,128)(2,1)S(1)} fusion(bf16[128,1,32,512]{3,0,2,1:T(8,128)(2,1)} %bitcast_dynamic-update-slice_fusion, bf16[128,32,32]{2,1,0:T(8,128)(2,1)S(1)} %reshape.164), kind=kOutput, calls=%fused_computation.20 | convolution fusion | flops 134234112 | bytes 4489216 | tf_op jit(solution)/shard_map/cab,can->bn/dot_general | solution.py:108
  260.4 0.0 copy-done
  260.4 0.0 copy-start.2
  260.4 0.7 fusion.30
  261.2 0.0 collective-permute-done
  261.2 0.0 collective-permute-done.1
  261.2 0.8 copy-done.2
  262.0 12.3 %fusion.4 = f32[1,1,2048,512]{3,2,1,0:T(8,128)} fusion(f32[512,2048]{0,1:T(8,128)S(1)} %fusion.30, f32[2048,512]{1,0:T(8,128)} %fusion.2, bf16[1,1,2048,2048]{3,2,1,0:T(8,128)(2,1)} %param.12, s32[]{:T(128)S(6)} %select_n.4, bf16[1,1,2048,512]{3,2,1,0:T(8,128)(2,1)} %collective-permute-done, bf16[1,1,2048,512]{3,2,1,0:T(8,128)(2,1)S(1)} %copy-done.2, ...), kind=kOutput, calls=%fused_computation.8 | convolution fusion | flops 4300210176 | bytes 27262984 | tf_op jit(solution)/shard_map/dot_general | solution.py:60
  (9 shorter events, 0.2 us)
Async XLA Ops:
  0.0 260.4 %copy-start = (bf16[1,1,2048,32]{2,3,1,0:T(8,128)(2,1)S(1)}, bf16[1,1,2048,32]{2,3,1,0:T(8,128)(2,1)}, u32[]{:S(2)}) copy-start(bf16[1,1,2048,32]{2,3,1,0:T(8,128)(2,1)} %param.14) | copy-start | bytes 393220
  0.0 20.0 %copy-start.1 = (bf16[1,1,2048,512]{3,2,1,0:T(8,128)(2,1)S(1)}, bf16[1,1,2048,512]{3,2,1,0:T(8,128)(2,1)}, u32[]{:S(2)}) copy-start(bf16[1,1,2048,512]{3,2,1,0:T(8,128)(2,1)} %param.10) | copy-start | bytes 6291460
  0.0 261.2 %collective-permute-start = (bf16[1,1,2048,512]{3,2,1,0:T(8,128)(2,1)}, bf16[1,1,2048,512]{3,2,1,0:T(8,128)(2,1)}, u32[]{:S(2)}, u32[]{:S(2)}) collective-permute-start(bf16[1,1,2048,512]{3,2,1,0:T(8,128)(2,1)} %param.10), channel_id=1, source_target_pairs={{0,8},{8,16},{16,24},{24,32},{32,40},{40,48},{48,56},{56,64},{64,7... | collective-permute-start | bytes 6291464 | tf_op jit(solution)/shard_map/ppermute | solution.py:18
  0.0 261.2 %collective-permute-start.1 = (bf16[1,1,2048,512]{3,2,1,0:T(8,128)(2,1)}, bf16[1,1,2048,512]{3,2,1,0:T(8,128)(2,1)}, u32[]{:S(2)}, u32[]{:S(2)}) collective-permute-start(bf16[1,1,2048,512]{3,2,1,0:T(8,128)(2,1)} %param.10), channel_id=1, source_target_pairs={{8,0},{16,8},{24,16},{32,24},{40,32},{48,40},{56,48},{64,56},{72,6... | collective-permute-start | bytes 6291464 | tf_op jit(solution)/shard_map/ppermute | solution.py:21
  11.8 243.6 %all-to-all-start = ((bf16[128,2,512]{2,1,0:T(2,128)(2,1)}), bf16[128,2,512]{2,1,0:T(2,128)(2,1)}, u32[]{:S(2)}, u32[]{:S(2)}) async-start(bf16[128,2,512]{2,1,0:T(2,128)(2,1)} %reshape.163), calls=%async_computation | async-start | bytes 524288 | tf_op jit(solution)/shard_map/all_to_all | solution.py:105
  260.4 1.6 copy-start.2
where the time goes:
time: 275 us; the launch traced here: 274 us
  blocking collectives  212 us (77%)
  matrix products  29.1 us (11%)
  local copies, waits for them, and re-layouts  16.6 us (6%)
  starting transfers between devices  13.5 us (5%)
    all_gather x25, blocking collectives, all_blocks(): pieces = lax.all_gather(pieces, axes[k], axis=0, tiled=True)  212 us
    dot_general x3, matrix products, contract(): lax.dot_general(tile, values, (((0,), (0,)), ((), ())), preferred_element...  24.2 us
    all_to_all x1, starting transfers between devices, on_device(): lax.all_to_all(coupled_blocks.astype(jnp.bfloat16), ROW_COL, split_axis=0...  8.18 us
    unnamed x12, local copies, waits for them, and re-layouts  8.06 us
  transfers between devices with their start and end apart: 3, of which 0 were waited for; matrix products, arithmetic and copies ran while one was open for 12% of the time, Pallas kernels for 0%

commit v1 on v0

--- a/solution.py
+++ b/solution.py
@@ -31,7 +31,16 @@
 def all_blocks(value, axes, sequence):
     pieces = value[None]
     for k in sequence:
-        pieces = lax.all_gather(pieces, axes[k], axis=0, tiled=True)
+        lane_scan = lambda field, comm_axis, axis_k: jnp.concatenate(
+            lax.all_to_all(
+                jnp.stack([field for _ in range(lax.axis_size(comm_axis))], axis=0),
+                concat_axis=0,
+                axis_name=comm_axis,
+                split_axis=0,
+            ),
+            axis=axis_k,
+        )
+        pieces = lane_scan(pieces, axes[k], 0)
     held = [lax.axis_size(axes[k]) for k in reversed(sequence)]
     pieces = pieces.reshape(*held, *value.shape)
     turned = sorted(range(len(sequence)), key=lambda place: sequence[len(sequence) - 1 - place])

time: 275 us -> 332 us (1.21)
  blocking collectives: 212 us -> 28.6 us
  waiting for transfers between devices: 0.01 us -> 121 us
  starting transfers between devices: 13.5 us -> 93.7 us
  local copies, waits for them, and re-layouts: 16.6 us -> 47.6 us
  other arithmetic: 1.67 us -> 6.76 us
    all_gather x25 -> x0, blocking collectives: 212 us -> none  [all_blocks(): pieces = lax.all_gather(pieces, axes[k], axis=0, tiled=True)]
    all_to_all x0 -> x20, waiting for transfers between devices: none -> 111 us  [all_blocks(): lax.all_to_all(jnp.stack([field for _ in range(lax.axis_size(comm_axis))]...]
    all_to_all x0 -> x20, starting transfers between devices: none -> 82 us  [all_blocks(): lax.all_to_all(jnp.stack([field for _ in range(lax.axis_size(comm_axis))]...]
    all_to_all x0 -> x5, blocking collectives: none -> 28.6 us  [all_blocks(): lax.all_to_all(jnp.stack([field for _ in range(lax.axis_size(comm_axis))]...]
    another operation x0 -> x23, local copies, waits for them, and re-layouts: none -> 11.2 us  [the longest x22 8.39 us: all_blocks(): jnp.stack([field for _ in range(lax.axis_size(comm_axis))], axis=0)]
    reshape x4, local copies, waits for them, and re-layouts: 1.25 us -> 11.3 us  [all_blocks(): pieces.transpose(*turned, *range(len(sequence), pieces.ndim))]
    all_to_all x1, waiting for transfers between devices: 0.01 us -> 9.67 us  [on_device(): lax.all_to_all(coupled_blocks.astype(jnp.bfloat16), ROW_COL, split_axis=0...]
    another operation x0 -> x15, other arithmetic: none -> 6.68 us  [all_blocks(): jnp.stack([field for _ in range(lax.axis_size(comm_axis))], axis=0)]
  transfers between devices with their start and end apart: 3 -> 23, of which waited for: 0 -> 19; matrix products, arithmetic and copies ran while one was open for 12% -> 19% of each run, Pallas kernels for 0% -> 0%
where the time goes in v1:
time: 332 us; the launch traced here: 328 us
  waiting for transfers between devices  121 us (36%)
  starting transfers between devices  93.7 us (28%)
  local copies, waits for them, and re-layouts  47.6 us (14%)
  matrix products  29.4 us (9%)
  blocking collectives  28.6 us (9%)
  other arithmetic  6.76 us (2%)
    all_to_all x20, waiting for transfers between devices, all_blocks(): lax.all_to_all(jnp.stack([field for _ in range(lax.axis_size(comm_axis))]...  111 us
    all_to_all x20, starting transfers between devices, all_blocks(): lax.all_to_all(jnp.stack([field for _ in range(lax.axis_size(comm_axis))]...  82 us
    all_to_all x5, blocking collectives, all_blocks(): lax.all_to_all(jnp.stack([field for _ in range(lax.axis_size(comm_axis))]...  28.6 us
    dot_general x3, matrix products, contract(): lax.dot_general(tile, values, (((0,), (0,)), ((), ())), preferred_element...  25.1 us
    reshape x4, local copies, waits for them, and re-layouts, all_blocks(): pieces.transpose(*turned, *range(len(sequence), pieces.ndim))  11.3 us
    unnamed x22, local copies, waits for them, and re-layouts  11.1 us
    all_to_all x1, waiting for transfers between devices, on_device(): lax.all_to_all(coupled_blocks.astype(jnp.bfloat16), ROW_COL, split_axis=0...  9.67 us
    another operation x22, local copies, waits for them, and re-layouts, all_blocks(): jnp.stack([field for _ in range(lax.axis_size(comm_axis))], axis=0)  8.39 us
  transfers between devices with their start and end apart: 23, of which 19 were waited for; matrix products, arithmetic and copies ran while one was open for 19% of the time, Pallas kernels for 0%

profile of v1, /device:TPU:40, one launch (start us, length us, event | category | flops | bytes accessed | tf_op | source)
XLA Modules:
  0.0 328.3 jit_solution(16167904188411604946)
XLA Ops:
  0.0 2.2 fusion.25
  2.8 3.2 all-to-all-start.11
  7.4 3.6 %all-to-all-start.1 = ((bf16[2,1,1,6,512]{4,3,2,1,0:T(8,128)(2,1)}), bf16[2,1,1,6,512]{4,3,2,1,0:T(8,128)(2,1)S(1)}, u32[]{:S(2)}, u32[]{:S(2)}) async-start(bf16[2,1,1,6,512]{4,3,2,1,0:T(8,128)(2,1)} %pad_maximum_fusion.12), calls=%async_computation.1 | async-start | bytes 32768 | tf_op jit(solution)/shard_map/all_to_all | solution.py:35
  11.6 4.8 %all-to-all-done.1 = bf16[2,1,1,6,512]{4,3,2,1,0:T(8,128)(2,1)S(1)} async-done(((bf16[2,1,1,6,512]{4,3,2,1,0:T(8,128)(2,1)}), bf16[2,1,1,6,512]{4,3,2,1,0:T(8,128)(2,1)S(1)}, u32[]{:S(2)}, u32[]{:S(2)}) %all-to-all-start.1) | async-done | bytes 12320 | tf_op jit(solution)/shard_map/all_to_all | solution.py:35
  16.4 4.6 %all-to-all-start.21 = ((bf16[2,1,1,7,512]{4,3,2,1,0:T(8,128)(2,1)}), bf16[2,1,1,7,512]{4,3,2,1,0:T(8,128)(2,1)S(1)}, u32[]{:S(2)}, u32[]{:S(2)}) async-start(bf16[2,1,1,7,512]{4,3,2,1,0:T(8,128)(2,1)} %pad_maximum_fusion.14), calls=%async_computation.21 | async-start | bytes 32768 | tf_op jit(solution)/shard_map/all_to_all | solution.py:35
  21.0 1.8 all-to-all-done.21
  22.8 6.2 %all_to_all.130 = bf16[2,2,1,6,512]{4,1,3,2,0:T(2,128)(2,1)S(1)} all-to-all(bf16[2,2,1,6,512]{4,1,3,2,0:T(2,128)(2,1)S(1)} %copy.86), channel_id=1, replica_groups=mesh['row_0'=2,'row_1'=4,'row_2'=2,'col_0'=4,'col_1'=2] {'col_1'}, dimensions={0} | all-to-all | bytes 49152 | tf_op jit(solution)/shard_map/all_to_all | solution.py:35
  29.0 9.5 %all_to_all.131 = bf16[4,1,1,6,512]{4,3,2,1,0:T(8,128)(2,1)S(1)} all-to-all(bf16[4,1,1,6,512]{4,3,2,1,0:T(8,128)(2,1)S(1)} %stack.80), channel_id=1, replica_groups=mesh['row_0'=2,'row_1'=4,'row_2'=2,'col_0'=4,'col_1'=2] {'row_1'}, dimensions={0} | all-to-all | bytes 49152 | tf_op jit(solution)/shard_map/all_to_all | solution.py:35
  39.2 5.4 %all-to-all-start.16 = ((bf16[4,1,1,6,512]{4,3,2,1,0:T(8,128)(2,1)}), bf16[4,1,1,6,512]{4,3,2,1,0:T(8,128)(2,1)S(1)}, u32[]{:S(2)}, u32[]{:S(2)}) async-start(bf16[4,1,1,6,512]{4,3,2,1,0:T(8,128)(2,1)} %stack.90), calls=%async_computation.16 | async-start | bytes 65536 | tf_op jit(solution)/shard_map/all_to_all | solution.py:35
  45.2 3.3 %all-to-all-done.16 = bf16[4,1,1,6,512]{4,3,2,1,0:T(8,128)(2,1)S(1)} async-done(((bf16[4,1,1,6,512]{4,3,2,1,0:T(8,128)(2,1)}), bf16[4,1,1,6,512]{4,3,2,1,0:T(8,128)(2,1)S(1)}, u32[]{:S(2)}, u32[]{:S(2)}) %all-to-all-start.16) | async-done | bytes 24608 | tf_op jit(solution)/shard_map/all_to_all | solution.py:35
  48.6 3.3 all-to-all-start.7
  52.5 4.8 %all-to-all-done.7 = bf16[2,4,1,6,512]{4,1,3,2,0:T(4,128)(2,1)S(1)} async-done(((bf16[2,4,1,6,512]{4,1,3,2,0:T(4,128)(2,1)}), bf16[2,4,1,6,512]{4,1,3,2,0:T(4,128)(2,1)S(1)}, u32[]{:S(2)}, u32[]{:S(2)}) %all-to-all-start.7) | async-done | bytes 49184 | tf_op jit(solution)/shard_map/all_to_all | solution.py:35
  58.0 3.3 all-to-all-start.12
  62.1 4.8 %all-to-all-done.12 = bf16[4,2,1,7,512]{4,1,3,2,0:T(2,128)(2,1)S(1)} async-done(((bf16[4,2,1,7,512]{4,1,3,2,0:T(2,128)(2,1)}), bf16[4,2,1,7,512]{4,1,3,2,0:T(2,128)(2,1)S(1)}, u32[]{:S(2)}, u32[]{:S(2)}) %all-to-all-start.12) | async-done | bytes 57376 | tf_op jit(solution)/shard_map/all_to_all | solution.py:35
  67.5 4.7 %all-to-all-start.22 = ((bf16[4,2,1,7,512]{4,1,3,2,0:T(2,128)(2,1)}), bf16[4,2,1,7,512]{4,1,3,2,0:T(2,128)(2,1)S(1)}, u32[]{:S(2)}, u32[]{:S(2)}) async-start(bf16[4,2,1,7,512]{4,1,3,2,0:T(2,128)(2,1)} %stack.96), calls=%async_computation.22 | async-start | bytes 114688 | tf_op jit(solution)/shard_map/all_to_all | solution.py:35
  72.9 3.4 %all-to-all-done.22 = bf16[4,2,1,7,512]{4,1,3,2,0:T(2,128)(2,1)S(1)} async-done(((bf16[4,2,1,7,512]{4,1,3,2,0:T(2,128)(2,1)}), bf16[4,2,1,7,512]{4,1,3,2,0:T(2,128)(2,1)S(1)}, u32[]{:S(2)}, u32[]{:S(2)}) %all-to-all-start.22) | async-done | bytes 57376 | tf_op jit(solution)/shard_map/all_to_all | solution.py:35
  77.0 4.7 %all-to-all-start.3 = ((bf16[4,4,1,6,512]{4,1,3,2,0:T(4,128)(2,1)}), bf16[4,4,1,6,512]{4,1,3,2,0:T(4,128)(2,1)S(1)}, u32[]{:S(2)}, u32[]{:S(2)}) async-start(bf16[4,4,1,6,512]{4,1,3,2,0:T(4,128)(2,1)} %stack.77), calls=%async_computation.3 | async-start | bytes 196608 | tf_op jit(solution)/shard_map/all_to_all | solution.py:35
  81.8 4.2 %all-to-all-done.3 = bf16[4,4,1,6,512]{4,1,3,2,0:T(4,128)(2,1)S(1)} async-done(((bf16[4,4,1,6,512]{4,1,3,2,0:T(4,128)(2,1)}), bf16[4,4,1,6,512]{4,1,3,2,0:T(4,128)(2,1)S(1)}, u32[]{:S(2)}, u32[]{:S(2)}) %all-to-all-start.3) | async-done | bytes 98336 | tf_op jit(solution)/shard_map/all_to_all | solution.py:35
  86.1 3.3 all-to-all-start.17
  89.5 1.3 all-to-all-done.17
  90.8 3.8 %all_to_all.132 = bf16[2,8,1,7,512]{4,1,3,2,0:T(8,128)(2,1)S(1)} all-to-all(bf16[2,8,1,7,512]{4,1,3,2,0:T(8,128)(2,1)S(1)} %pad_maximum_fusion.7), channel_id=1, replica_groups=mesh['row_0'=2,'row_1'=4,'row_2'=2,'col_0'=4,'col_1'=2] {'row_2'}, dimensions={0} | all-to-all | bytes 229376 | tf_op jit(solution)/shard_map/all_to_all | solution.py:35
  94.6 3.9 %all_to_all.133 = bf16[2,16,1,6,512]{4,1,3,2,0:T(8,128)(2,1)S(1)} all-to-all(bf16[2,16,1,6,512]{4,1,3,2,0:T(8,128)(2,1)S(1)} %pad_maximum_fusion.5), channel_id=1, replica_groups=mesh['row_0'=2,'row_1'=4,'row_2'=2,'col_0'=4,'col_1'=2] {'row_2'}, dimensions={0} | all-to-all | bytes 393216 | tf_op jit(solution)/shard_map/all_to_all | solution.py:35
  98.5 5.3 %all-to-all-start.8 = ((bf16[2,8,1,6,512]{4,1,3,2,0:T(8,128)(2,1)}), bf16[2,8,1,6,512]{4,1,3,2,0:T(8,128)(2,1)S(1)}, u32[]{:S(2)}, u32[]{:S(2)}) async-start(bf16[2,8,1,6,512]{4,1,3,2,0:T(8,128)(2,1)} %pad_maximum_fusion.8), calls=%async_computation.8 | async-start | bytes 196608 | tf_op jit(solution)/shard_map/all_to_all | solution.py:35
  104.4 1.6 all-to-all-done.8
  106.1 3.4 %all-to-all-start.13 = ((bf16[2,8,1,7,512]{4,1,3,2,0:T(8,128)(2,1)}), bf16[2,8,1,7,512]{4,1,3,2,0:T(8,128)(2,1)S(1)}, u32[]{:S(2)}, u32[]{:S(2)}) async-start(bf16[2,8,1,7,512]{4,1,3,2,0:T(8,128)(2,1)} %pad_maximum_fusion.6), calls=%async_computation.13 | async-start | bytes 229376 | tf_op jit(solution)/shard_map/all_to_all | solution.py:35
  109.5 5.8 %all-to-all-done.13 = bf16[2,8,1,7,512]{4,1,3,2,0:T(8,128)(2,1)S(1)} async-done(((bf16[2,8,1,7,512]{4,1,3,2,0:T(8,128)(2,1)}), bf16[2,8,1,7,512]{4,1,3,2,0:T(8,128)(2,1)S(1)}, u32[]{:S(2)}, u32[]{:S(2)}) %all-to-all-start.13) | async-done | bytes 114720 | tf_op jit(solution)/shard_map/all_to_all | solution.py:35
  116.0 3.4 %all-to-all-start.18 = ((bf16[4,8,1,6,512]{4,1,3,2,0:T(8,128)(2,1)}), bf16[4,8,1,6,512]{4,1,3,2,0:T(8,128)(2,1)S(1)}, u32[]{:S(2)}, u32[]{:S(2)}) async-start(bf16[4,8,1,6,512]{4,1,3,2,0:T(8,128)(2,1)} %stack.92), calls=%async_computation.18 | async-start | bytes 393216 | tf_op jit(solution)/shard_map/all_to_all | solution.py:35
  120.2 5.5 %all-to-all-done.18 = bf16[4,8,1,6,512]{4,1,3,2,0:T(8,128)(2,1)S(1)} async-done(((bf16[4,8,1,6,512]{4,1,3,2,0:T(8,128)(2,1)}), bf16[4,8,1,6,512]{4,1,3,2,0:T(8,128)(2,1)S(1)}, u32[]{:S(2)}, u32[]{:S(2)}) %all-to-all-start.18) | async-done | bytes 196640 | tf_op jit(solution)/shard_map/all_to_all | solution.py:35
  125.7 5.4 %all-to-all-start.14 = ((bf16[2,16,1,7,512]{4,1,3,2,0:T(8,128)(2,1)}), bf16[2,16,1,7,512]{4,1,3,2,0:T(8,128)(2,1)S(1)}, u32[]{:S(2)}, u32[]{:S(2)}) async-start(bf16[2,16,1,7,512]{4,1,3,2,0:T(8,128)(2,1)} %pad_maximum_fusion.4), calls=%async_computation.14 | async-start | bytes 458752 | tf_op jit(solution)/shard_map/all_to_all | solution.py:35
  131.6 1.4 copy.85
  133.0 1.5 reshape.156
  134.5 6.2 %all-to-all-start = ((bf16[128,2,512]{2,1,0:T(2,128)(2,1)}), bf16[128,2,512]{2,1,0:T(2,128)(2,1)S(1)}, u32[]{:S(2)}, u32[]{:S(2)}) async-start(bf16[128,2,512]{2,1,0:T(2,128)(2,1)} %reshape.156), calls=%async_computation | async-start | bytes 524288 | tf_op jit(solution)/shard_map/all_to_all | solution.py:114
  140.8 9.7 %all-to-all-done = bf16[128,2,512]{2,1,0:T(2,128)(2,1)S(1)} async-done(((bf16[128,2,512]{2,1,0:T(2,128)(2,1)}), bf16[128,2,512]{2,1,0:T(2,128)(2,1)S(1)}, u32[]{:S(2)}, u32[]{:S(2)}) %all-to-all-start) | async-done | bytes 262176 | tf_op jit(solution)/shard_map/all_to_all | solution.py:114
  151.2 4.6 %all-to-all-start.9 = ((bf16[4,16,1,6,512]{4,1,3,2,0:T(8,128)(2,1)}), bf16[4,16,1,6,512]{4,1,3,2,0:T(8,128)(2,1)S(1)}, u32[]{:S(2)}, u32[]{:S(2)}) async-start(bf16[4,16,1,6,512]{4,1,3,2,0:T(8,128)(2,1)} %stack.83), calls=%async_computation.9 | async-start | bytes 786432 | tf_op jit(solution)/shard_map/all_to_all | solution.py:35
  156.6 5.3 %all-to-all-done.9 = bf16[4,16,1,6,512]{4,1,3,2,0:T(8,128)(2,1)S(1)} async-done(((bf16[4,16,1,6,512]{4,1,3,2,0:T(8,128)(2,1)}), bf16[4,16,1,6,512]{4,1,3,2,0:T(8,128)(2,1)S(1)}, u32[]{:S(2)}, u32[]{:S(2)}) %all-to-all-start.9) | async-done | bytes 393248 | tf_op jit(solution)/shard_map/all_to_all | solution.py:35
  161.9 3.5 %all-to-all-start.19 = ((bf16[2,32,1,6,512]{4,1,3,2,0:T(8,128)(2,1)}), bf16[2,32,1,6,512]{4,1,3,2,0:T(8,128)(2,1)S(1)}, u32[]{:S(2)}, u32[]{:S(2)}) async-start(bf16[2,32,1,6,512]{4,1,3,2,0:T(8,128)(2,1)} %pad_maximum_fusion.3), calls=%async_computation.19 | async-start | bytes 786432 | tf_op jit(solution)/shard_map/all_to_all | solution.py:35
  165.5 7.2 %all-to-all-done.19 = bf16[2,32,1,6,512]{4,1,3,2,0:T(8,128)(2,1)S(1)} async-done(((bf16[2,32,1,6,512]{4,1,3,2,0:T(8,128)(2,1)}), bf16[2,32,1,6,512]{4,1,3,2,0:T(8,128)(2,1)S(1)}, u32[]{:S(2)}, u32[]{:S(2)}) %all-to-all-start.19) | async-done | bytes 393248 | tf_op jit(solution)/shard_map/all_to_all | solution.py:35
  172.8 5.1 %all_to_all.134 = bf16[2,64,1,6,512]{4,1,3,2,0:T(8,128)(2,1)} all-to-all(bf16[2,64,1,6,512]{4,1,3,2,0:T(8,128)(2,1)S(1)} %pad_maximum_fusion.1), channel_id=1, replica_groups=mesh['row_0'=2,'row_1'=4,'row_2'=2,'col_0'=4,'col_1'=2] {'row_2'}, dimensions={0} | all-to-all | bytes 1572864 | tf_op jit(solution)/shard_map/all_to_all | solution.py:35
  178.7 3.5 %all-to-all-start.24 = ((bf16[4,16,1,7,512]{4,1,3,2,0:T(8,128)(2,1)}), bf16[4,16,1,7,512]{4,1,3,2,0:T(8,128)(2,1)S(1)}, u32[]{:S(2)}, u32[]{:S(2)}) async-start(bf16[4,16,1,7,512]{4,1,3,2,0:T(8,128)(2,1)} %stack.98), calls=%async_computation.24 | async-start | bytes 917504 | tf_op jit(solution)/shard_map/all_to_all | solution.py:35
  182.2 9.3 %all-to-all-done.24 = bf16[4,16,1,7,512]{4,1,3,2,0:T(8,128)(2,1)S(1)} async-done(((bf16[4,16,1,7,512]{4,1,3,2,0:T(8,128)(2,1)}), bf16[4,16,1,7,512]{4,1,3,2,0:T(8,128)(2,1)S(1)}, u32[]{:S(2)}, u32[]{:S(2)}) %all-to-all-start.24) | async-done | bytes 458784 | tf_op jit(solution)/shard_map/all_to_all | solution.py:35
  192.5 3.5 %all-to-all-start.5 = ((bf16[4,32,1,6,512]{4,1,3,2,0:T(8,128)(2,1)}), bf16[4,32,1,6,512]{4,1,3,2,0:T(8,128)(2,1)S(1)}, u32[]{:S(2)}, u32[]{:S(2)}) async-start(bf16[4,32,1,6,512]{4,1,3,2,0:T(8,128)(2,1)} %stack.79), calls=%async_computation.5 | async-start | bytes 1572864 | tf_op jit(solution)/shard_map/all_to_all | solution.py:35
  197.0 11.0 %all-to-all-done.5 = bf16[4,32,1,6,512]{4,1,3,2,0:T(8,128)(2,1)S(1)} async-done(((bf16[4,32,1,6,512]{4,1,3,2,0:T(8,128)(2,1)}), bf16[4,32,1,6,512]{4,1,3,2,0:T(8,128)(2,1)S(1)}, u32[]{:S(2)}, u32[]{:S(2)}) %all-to-all-start.5) | async-done | bytes 786464 | tf_op jit(solution)/shard_map/all_to_all | solution.py:35
  208.0 5.0 %all-to-all-start.20 = ((bf16[2,64,1,6,512]{4,1,3,2,0:T(8,128)(2,1)}), bf16[2,64,1,6,512]{4,1,3,2,0:T(8,128)(2,1)S(1)}, u32[]{:S(2)}, u32[]{:S(2)}) async-start(bf16[2,64,1,6,512]{4,1,3,2,0:T(8,128)(2,1)} %pad_maximum_fusion.2), calls=%async_computation.20 | async-start | bytes 1572864 | tf_op jit(solution)/shard_map/all_to_all | solution.py:35
  214.0 6.9 %all-to-all-done.20 = bf16[2,64,1,6,512]{4,1,3,2,0:T(8,128)(2,1)S(1)} async-done(((bf16[2,64,1,6,512]{4,1,3,2,0:T(8,128)(2,1)}), bf16[2,64,1,6,512]{4,1,3,2,0:T(8,128)(2,1)S(1)}, u32[]{:S(2)}, u32[]{:S(2)}) %all-to-all-start.20) | async-done | bytes 786464 | tf_op jit(solution)/shard_map/all_to_all | solution.py:35
  221.8 3.6 %all-to-all-start.25 = ((bf16[2,64,1,7,512]{4,1,3,2,0:T(8,128)(2,1)}), bf16[2,64,1,7,512]{4,1,3,2,0:T(8,128)(2,1)S(1)}, u32[]{:S(2)}, u32[]{:S(2)}) async-start(bf16[2,64,1,7,512]{4,1,3,2,0:T(8,128)(2,1)} %pad_maximum_fusion), calls=%async_computation.25 | async-start | bytes 1835008 | tf_op jit(solution)/shard_map/all_to_all | solution.py:35
  225.4 5.3 %collective-permute-start.1 = (bf16[1,1,2048,512]{3,2,1,0:T(8,128)(2,1)}, bf16[1,1,2048,512]{3,2,1,0:T(8,128)(2,1)}, u32[]{:S(2)}, u32[]{:S(2)}) collective-permute-start(bf16[1,1,2048,512]{3,2,1,0:T(8,128)(2,1)} %param.10), channel_id=1, source_target_pairs={{8,0},{16,8},{24,16},{32,24},{40,32},{48,40},{56,48},{64,56},{72,6... | collective-permute-start | bytes 6291464 | tf_op jit(solution)/shard_map/ppermute | solution.py:21
  230.8 29.0 %all-to-all-done.25 = bf16[2,64,1,7,512]{4,1,3,2,0:T(8,128)(2,1)S(1)} async-done(((bf16[2,64,1,7,512]{4,1,3,2,0:T(8,128)(2,1)}), bf16[2,64,1,7,512]{4,1,3,2,0:T(8,128)(2,1)S(1)}, u32[]{:S(2)}, u32[]{:S(2)}) %all-to-all-start.25) | async-done | bytes 917536 | tf_op jit(solution)/shard_map/all_to_all | solution.py:35
  260.8 4.9 %all-to-all-start.15 = ((bf16[4,32,1,7,512]{4,1,3,2,0:T(8,128)(2,1)}), bf16[4,32,1,7,512]{4,1,3,2,0:T(8,128)(2,1)S(1)}, u32[]{:S(2)}, u32[]{:S(2)}) async-start(bf16[4,32,1,7,512]{4,1,3,2,0:T(8,128)(2,1)} %stack.89), calls=%async_computation.15 | async-start | bytes 1835008 | tf_op jit(solution)/shard_map/all_to_all | solution.py:35
  265.8 10.6 %fusion.2 = f32[2048,512]{1,0:T(8,128)} fusion(bf16[1,1,2048,2048]{3,2,1,0:T(8,128)(2,1)} %param.11, bf16[1,1,2048,512]{3,2,1,0:T(8,128)(2,1)} %param.10), kind=kOutput, calls=%fused_computation.2 | convolution fusion | flops 4294967296 | bytes 14680064 | tf_op jit(solution)/shard_map/dot_general | solution.py:69
  277.5 1.9 copy.96
  279.4 1.7 copy.97
  281.1 3.0 reshape.148
  284.1 1.7 copy.90
  285.8 1.7 copy.91
  287.6 2.9 reshape.147
  290.5 2.1 constant_dynamic-update-slice_fusion.4
  292.6 2.1 constant_dynamic-update-slice_fusion.3
  294.7 2.8 copy.118
  297.6 3.0 reshape.150
  302.3 2.3 copy.103
  304.6 2.5 reshape.149
  308.1 2.1 constant_dynamic-update-slice_fusion.1
  311.2 3.1 fusion.19
  315.9 12.3 %fusion.4 = f32[1,1,2048,512]{3,2,1,0:T(8,128)} fusion(f32[512,2048]{0,1:T(8,128)S(1)} %fusion.30, f32[2048,512]{1,0:T(8,128)} %fusion.2, bf16[1,1,2048,2048]{3,2,1,0:T(8,128)(2,1)} %param.12, s32[]{:T(128)S(6)} %select_n.4, bf16[1,1,2048,512]{3,2,1,0:T(8,128)(2,1)} %collective-permute-done, bf16[1,1,2048,512]{3,2,1,0:T(8,128)(2,1)S(1)} %copy-done.4, ...), kind=kOutput, calls=%fused_computation.8 | convolution fusion | flops 4300210176 | bytes 27262984 | tf_op jit(solution)/shard_map/dot_general | solution.py:69
  (85 shorter events, 23.5 us)
Async XLA Ops:
  0.0 314.3 %copy-start = (bf16[1,1,2048,32]{2,3,1,0:T(8,128)(2,1)S(1)}, bf16[1,1,2048,32]{2,3,1,0:T(8,128)(2,1)}, u32[]{:S(2)}) copy-start(bf16[1,1,2048,32]{2,3,1,0:T(8,128)(2,1)} %param.14) | copy-start | bytes 393220
  0.0 119.4 %copy-start.6 = (s32[1,1,64]{2,1,0:T(1,128)S(1)}, s32[1,1,64]{2,1,0:T(1,128)}, u32[]{:S(2)}) copy-start(s32[1,1,64]{2,1,0:T(1,128)} %param.18) | copy-start | bytes 772
  0.0 119.4 %copy-start.5 = (bf16[1,1,64,32,32]{2,4,3,1,0:T(8,128)(2,1)S(1)}, bf16[1,1,64,32,32]{2,4,3,1,0:T(8,128)(2,1)}, u32[]{:S(2)}) copy-start(bf16[1,1,64,32,32]{2,4,3,1,0:T(8,128)(2,1)} %param.15) | copy-start | bytes 393220
  2.2 128.9 %copy-start.7 = (s32[1,1,64]{2,1,0:T(1,128)S(1)}, s32[1,1,64]{2,1,0:T(1,128)}, u32[]{:S(2)}) copy-start(s32[1,1,64]{2,1,0:T(1,128)} %param.17) | copy-start | bytes 772
  2.8 4.6 %all-to-all-start.11 = ((bf16[2,1,1,7,512]{4,3,2,1,0:T(8,128)(2,1)}), bf16[2,1,1,7,512]{4,3,2,1,0:T(8,128)(2,1)S(1)}, u32[]{:S(2)}, u32[]{:S(2)}) async-start(bf16[2,1,1,7,512]{4,3,2,1,0:T(8,128)(2,1)} %pad_maximum_fusion.13), calls=%async_computation.11 | async-start | bytes 32768 | tf_op jit(solution)/shard_map/all_to_all | solution.py:35
  7.4 8.9 %all-to-all-start.1 = ((bf16[2,1,1,6,512]{4,3,2,1,0:T(8,128)(2,1)}), bf16[2,1,1,6,512]{4,3,2,1,0:T(8,128)(2,1)S(1)}, u32[]{:S(2)}, u32[]{:S(2)}) async-start(bf16[2,1,1,6,512]{4,3,2,1,0:T(8,128)(2,1)} %pad_maximum_fusion.12), calls=%async_computation.1 | async-start | bytes 32768 | tf_op jit(solution)/shard_map/all_to_all | solution.py:35
  16.4 6.4 %all-to-all-start.21 = ((bf16[2,1,1,7,512]{4,3,2,1,0:T(8,128)(2,1)}), bf16[2,1,1,7,512]{4,3,2,1,0:T(8,128)(2,1)S(1)}, u32[]{:S(2)}, u32[]{:S(2)}) async-start(bf16[2,1,1,7,512]{4,3,2,1,0:T(8,128)(2,1)} %pad_maximum_fusion.14), calls=%async_computation.21 | async-start | bytes 32768 | tf_op jit(solution)/shard_map/all_to_all | solution.py:35
  39.2 9.4 %all-to-all-start.16 = ((bf16[4,1,1,6,512]{4,3,2,1,0:T(8,128)(2,1)}), bf16[4,1,1,6,512]{4,3,2,1,0:T(8,128)(2,1)S(1)}, u32[]{:S(2)}, u32[]{:S(2)}) async-start(bf16[4,1,1,6,512]{4,3,2,1,0:T(8,128)(2,1)} %stack.90), calls=%async_computation.16 | async-start | bytes 65536 | tf_op jit(solution)/shard_map/all_to_all | solution.py:35
  48.6 8.8 %all-to-all-start.7 = ((bf16[2,4,1,6,512]{4,1,3,2,0:T(4,128)(2,1)}), bf16[2,4,1,6,512]{4,1,3,2,0:T(4,128)(2,1)S(1)}, u32[]{:S(2)}, u32[]{:S(2)}) async-start(bf16[2,4,1,6,512]{4,1,3,2,0:T(4,128)(2,1)} %copy.92), calls=%async_computation.7 | async-start | bytes 98304 | tf_op jit(solution)/shard_map/all_to_all | solution.py:35
  58.0 8.8 %all-to-all-start.12 = ((bf16[4,2,1,7,512]{4,1,3,2,0:T(2,128)(2,1)}), bf16[4,2,1,7,512]{4,1,3,2,0:T(2,128)(2,1)S(1)}, u32[]{:S(2)}, u32[]{:S(2)}) async-start(bf16[4,2,1,7,512]{4,1,3,2,0:T(2,128)(2,1)} %stack.86), calls=%async_computation.12 | async-start | bytes 114688 | tf_op jit(solution)/shard_map/all_to_all | solution.py:35
  67.5 8.8 %all-to-all-start.22 = ((bf16[4,2,1,7,512]{4,1,3,2,0:T(2,128)(2,1)}), bf16[4,2,1,7,512]{4,1,3,2,0:T(2,128)(2,1)S(1)}, u32[]{:S(2)}, u32[]{:S(2)}) async-start(bf16[4,2,1,7,512]{4,1,3,2,0:T(2,128)(2,1)} %stack.96), calls=%async_computation.22 | async-start | bytes 114688 | tf_op jit(solution)/shard_map/all_to_all | solution.py:35
  77.0 9.1 %all-to-all-start.3 = ((bf16[4,4,1,6,512]{4,1,3,2,0:T(4,128)(2,1)}), bf16[4,4,1,6,512]{4,1,3,2,0:T(4,128)(2,1)S(1)}, u32[]{:S(2)}, u32[]{:S(2)}) async-start(bf16[4,4,1,6,512]{4,1,3,2,0:T(4,128)(2,1)} %stack.77), calls=%async_computation.3 | async-start | bytes 196608 | tf_op jit(solution)/shard_map/all_to_all | solution.py:35
  86.1 4.7 %all-to-all-start.17 = ((bf16[2,4,1,6,512]{4,1,3,2,0:T(4,128)(2,1)}), bf16[2,4,1,6,512]{4,1,3,2,0:T(4,128)(2,1)S(1)}, u32[]{:S(2)}, u32[]{:S(2)}) async-start(bf16[2,4,1,6,512]{4,1,3,2,0:T(4,128)(2,1)} %copy.104), calls=%async_computation.17 | async-start | bytes 98304 | tf_op jit(solution)/shard_map/all_to_all | solution.py:35
  98.5 7.6 %all-to-all-start.8 = ((bf16[2,8,1,6,512]{4,1,3,2,0:T(8,128)(2,1)}), bf16[2,8,1,6,512]{4,1,3,2,0:T(8,128)(2,1)S(1)}, u32[]{:S(2)}, u32[]{:S(2)}) async-start(bf16[2,8,1,6,512]{4,1,3,2,0:T(8,128)(2,1)} %pad_maximum_fusion.8), calls=%async_computation.8 | async-start | bytes 196608 | tf_op jit(solution)/shard_map/all_to_all | solution.py:35
  106.1 9.2 %all-to-all-start.13 = ((bf16[2,8,1,7,512]{4,1,3,2,0:T(8,128)(2,1)}), bf16[2,8,1,7,512]{4,1,3,2,0:T(8,128)(2,1)S(1)}, u32[]{:S(2)}, u32[]{:S(2)}) async-start(bf16[2,8,1,7,512]{4,1,3,2,0:T(8,128)(2,1)} %pad_maximum_fusion.6), calls=%async_computation.13 | async-start | bytes 229376 | tf_op jit(solution)/shard_map/all_to_all | solution.py:35
  116.0 9.7 %all-to-all-start.18 = ((bf16[4,8,1,6,512]{4,1,3,2,0:T(8,128)(2,1)}), bf16[4,8,1,6,512]{4,1,3,2,0:T(8,128)(2,1)S(1)}, u32[]{:S(2)}, u32[]{:S(2)}) async-start(bf16[4,8,1,6,512]{4,1,3,2,0:T(8,128)(2,1)} %stack.92), calls=%async_computation.18 | async-start | bytes 393216 | tf_op jit(solution)/shard_map/all_to_all | solution.py:35
  125.7 8.9 %all-to-all-start.14 = ((bf16[2,16,1,7,512]{4,1,3,2,0:T(8,128)(2,1)}), bf16[2,16,1,7,512]{4,1,3,2,0:T(8,128)(2,1)S(1)}, u32[]{:S(2)}, u32[]{:S(2)}) async-start(bf16[2,16,1,7,512]{4,1,3,2,0:T(8,128)(2,1)} %pad_maximum_fusion.4), calls=%async_computation.14 | async-start | bytes 458752 | tf_op jit(solution)/shard_map/all_to_all | solution.py:35
  134.5 15.9 %all-to-all-start = ((bf16[128,2,512]{2,1,0:T(2,128)(2,1)}), bf16[128,2,512]{2,1,0:T(2,128)(2,1)S(1)}, u32[]{:S(2)}, u32[]{:S(2)}) async-start(bf16[128,2,512]{2,1,0:T(2,128)(2,1)} %reshape.156), calls=%async_computation | async-start | bytes 524288 | tf_op jit(solution)/shard_map/all_to_all | solution.py:114
  151.2 10.7 %all-to-all-start.9 = ((bf16[4,16,1,6,512]{4,1,3,2,0:T(8,128)(2,1)}), bf16[4,16,1,6,512]{4,1,3,2,0:T(8,128)(2,1)S(1)}, u32[]{:S(2)}, u32[]{:S(2)}) async-start(bf16[4,16,1,6,512]{4,1,3,2,0:T(8,128)(2,1)} %stack.83), calls=%async_computation.9 | async-start | bytes 786432 | tf_op jit(solution)/shard_map/all_to_all | solution.py:35
  161.9 10.8 %all-to-all-start.19 = ((bf16[2,32,1,6,512]{4,1,3,2,0:T(8,128)(2,1)}), bf16[2,32,1,6,512]{4,1,3,2,0:T(8,128)(2,1)S(1)}, u32[]{:S(2)}, u32[]{:S(2)}) async-start(bf16[2,32,1,6,512]{4,1,3,2,0:T(8,128)(2,1)} %pad_maximum_fusion.3), calls=%async_computation.19 | async-start | bytes 786432 | tf_op jit(solution)/shard_map/all_to_all | solution.py:35
  178.7 12.8 %all-to-all-start.24 = ((bf16[4,16,1,7,512]{4,1,3,2,0:T(8,128)(2,1)}), bf16[4,16,1,7,512]{4,1,3,2,0:T(8,128)(2,1)S(1)}, u32[]{:S(2)}, u32[]{:S(2)}) async-start(bf16[4,16,1,7,512]{4,1,3,2,0:T(8,128)(2,1)} %stack.98), calls=%async_computation.24 | async-start | bytes 917504 | tf_op jit(solution)/shard_map/all_to_all | solution.py:35
  192.5 15.5 %all-to-all-start.5 = ((bf16[4,32,1,6,512]{4,1,3,2,0:T(8,128)(2,1)}), bf16[4,32,1,6,512]{4,1,3,2,0:T(8,128)(2,1)S(1)}, u32[]{:S(2)}, u32[]{:S(2)}) async-start(bf16[4,32,1,6,512]{4,1,3,2,0:T(8,128)(2,1)} %stack.79), calls=%async_computation.5 | async-start | bytes 1572864 | tf_op jit(solution)/shard_map/all_to_all | solution.py:35
  208.0 12.9 %copy-start.2 = (bf16[4,32,1,6,512]{4,1,3,2,0:T(8,128)(2,1)}, bf16[4,32,1,6,512]{4,1,3,2,0:T(8,128)(2,1)S(1)}, u32[]{:S(2)}) copy-start(bf16[4,32,1,6,512]{4,1,3,2,0:T(8,128)(2,1)S(1)} %all-to-all-done.5) | copy-start | bytes 2359300
  208.0 12.9 %all-to-all-start.20 = ((bf16[2,64,1,6,512]{4,1,3,2,0:T(8,128)(2,1)}), bf16[2,64,1,6,512]{4,1,3,2,0:T(8,128)(2,1)S(1)}, u32[]{:S(2)}, u32[]{:S(2)}) async-start(bf16[2,64,1,6,512]{4,1,3,2,0:T(8,128)(2,1)} %pad_maximum_fusion.2), calls=%async_computation.20 | async-start | bytes 1572864 | tf_op jit(solution)/shard_map/all_to_all | solution.py:35
  220.9 0.9 copy-start.3
  221.8 38.0 %all-to-all-start.25 = ((bf16[2,64,1,7,512]{4,1,3,2,0:T(8,128)(2,1)}), bf16[2,64,1,7,512]{4,1,3,2,0:T(8,128)(2,1)S(1)}, u32[]{:S(2)}, u32[]{:S(2)}) async-start(bf16[2,64,1,7,512]{4,1,3,2,0:T(8,128)(2,1)} %pad_maximum_fusion), calls=%async_computation.25 | async-start | bytes 1835008 | tf_op jit(solution)/shard_map/all_to_all | solution.py:35
  225.4 89.7 %collective-permute-start = (bf16[1,1,2048,512]{3,2,1,0:T(8,128)(2,1)}, bf16[1,1,2048,512]{3,2,1,0:T(8,128)(2,1)}, u32[]{:S(2)}, u32[]{:S(2)}) collective-permute-start(bf16[1,1,2048,512]{3,2,1,0:T(8,128)(2,1)} %param.10), channel_id=1, source_target_pairs={{0,8},{8,16},{16,24},{24,32},{32,40},{40,48},{48,56},{56,64},{64,7... | collective-permute-start | bytes 6291464 | tf_op jit(solution)/shard_map/ppermute | solution.py:18
  225.4 89.7 %collective-permute-start.1 = (bf16[1,1,2048,512]{3,2,1,0:T(8,128)(2,1)}, bf16[1,1,2048,512]{3,2,1,0:T(8,128)(2,1)}, u32[]{:S(2)}, u32[]{:S(2)}) collective-permute-start(bf16[1,1,2048,512]{3,2,1,0:T(8,128)(2,1)} %param.10), channel_id=1, source_target_pairs={{8,0},{16,8},{24,16},{32,24},{40,32},{48,40},{56,48},{64,56},{72,6... | collective-permute-start | bytes 6291464 | tf_op jit(solution)/shard_map/ppermute | solution.py:21
  260.8 40.7 %all-to-all-start.15 = ((bf16[4,32,1,7,512]{4,1,3,2,0:T(8,128)(2,1)}), bf16[4,32,1,7,512]{4,1,3,2,0:T(8,128)(2,1)S(1)}, u32[]{:S(2)}, u32[]{:S(2)}) async-start(bf16[4,32,1,7,512]{4,1,3,2,0:T(8,128)(2,1)} %stack.89), calls=%async_computation.15 | async-start | bytes 1835008 | tf_op jit(solution)/shard_map/all_to_all | solution.py:35
  301.6 8.6 %copy-start.1 = (bf16[2,64,1,7,512]{4,1,0,3,2:T(8,128)(2,1)S(1)}, bf16[2,64,1,7,512]{4,1,0,3,2:T(8,128)(2,1)}, u32[]{:S(2)}) copy-start(bf16[2,64,1,7,512]{4,1,0,3,2:T(8,128)(2,1)} %copy.113) | copy-start | bytes 2752516
  314.3 1.6 copy-start.4
